TPU v7x, 32 devices: a whole 2x2x4 slice. The times are simulated.
32 devices in a mesh: dp: 2 (over x), tp: 16 (over y, z, core).
Axes of the slice: x: 2, y: 2, z: 4, core: 2. Of those that a mesh axis runs over, the one named last changes fastest.
Arguments:
- x: bfloat16 [4096, 5120], P('dp'), parts along dimension 0
- dy: bfloat16 [4096, 5120], P('dp'), parts along dimension 0
- gate: bfloat16 [4096, 14336], P('dp', 'tp'), parts along dimension 0
- up: bfloat16 [4096, 14336], P('dp', 'tp'), parts along dimension 0
- w_gate: bfloat16 [5120, 14336], P(None, 'tp')
- w_up: bfloat16 [5120, 14336], P(None, 'tp')
- w_down: bfloat16 [14336, 5120], P('tp')
Outputs:
- output 1: bfloat16 [4096, 5120], P('dp'), parts along dimension 0
- output 2: bfloat16 [10240, 14336], P('dp', 'tp'), parts along dimension 0
- output 3: bfloat16 [10240, 14336], P('dp', 'tp'), parts along dimension 0
- output 4: bfloat16 [28672, 5120], P(('dp', 'tp')), parts along dimension 0
There are 2 independent parts. A program takes and returns all parts, laid end to end along the dimension named above; an argument that names none is the same for every part.
All inputs are finite; a program needn't handle non-finite values.
Results may differ from a plain program's by a relative error of at most 0.012.
Values are sent between devices in bfloat16 or wider.
A program may use at most 2 GiB of HBM per device.

v0:
```python
import jax
import jax.numpy as jnp
from jax import lax
from jax.sharding import PartitionSpec as P


def act(gate, up):
    return jax.nn.silu(gate) * up


def solution(mesh):
    def step(x, dy, gate, up, w_gate, w_up, w_down):
        hidden, back = jax.vjp(act, gate.astype(jnp.float32), up.astype(jnp.float32))
        d_hidden = jnp.dot(dy, w_down.T, preferred_element_type=jnp.float32)
        d_gate, d_up = (g.astype(jnp.bfloat16) for g in back(d_hidden))
        term = jnp.dot(d_gate, w_gate.T, preferred_element_type=jnp.float32) + jnp.dot(d_up, w_up.T, preferred_element_type=jnp.float32)
        dx = lax.psum(term.astype(jnp.bfloat16), "tp")
        dw_gate = jnp.dot(x.T, d_gate, preferred_element_type=jnp.float32)
        dw_up = jnp.dot(x.T, d_up, preferred_element_type=jnp.float32)
        dw_down = jnp.dot(hidden.astype(jnp.bfloat16).T, dy, preferred_element_type=jnp.float32)
        return dx, *(g.astype(jnp.bfloat16) for g in (dw_gate, dw_up, dw_down))

    tokens, columns, rows = P("dp", None), P(None, "tp"), P("tp", None)
    return jax.shard_map(
        step,
        mesh=mesh,
        in_specs=(tokens, tokens, P("dp", "tp"), P("dp", "tp"), columns, columns, rows),
        out_specs=(tokens, P("dp", "tp"), P("dp", "tp"), P(("dp", "tp"), None)),
        check_vma=False,
    )
```

profile of v0, /device:TPU:0, one launch (start us, length us, event | category | flops | bytes accessed | tf_op | source)
XLA Modules:
  0.0 492.8 jit_solution(15293738236804589452)
XLA Ops:
  7.2 0.0 all-reduce.2.cloned.1.call-start
  7.2 31.4 %fusion.6 = (bf16[2048,896]{1,0:T(8,128)(2,1)S(1)}, f32[2048,896]{1,0:T(8,128)}) fusion(bf16[2048,896]{1,0:T(8,128)(2,1)} %param.9, bf16[2048,896]{1,0:T(8,128)(2,1)} %param.10, bf16[2048,5120]{1,0:T(8,128)(2,1)} %param.8, bf16[896,5120]{1,0:T(8,128)(2,1)} %param.13), kind=kOutput, calls=%fused_computation.16 | convolution fusion | flops 18814337024 | bytes 48496640 | tf_op jit(solution)/shard_map/dot_general | solution.py:14
  38.6 0.0 copy-start
  38.6 30.0 %fusion.9 = f32[2048,5120]{1,0:T(8,128)} fusion(bf16[2048,896]{1,0:T(8,128)(2,1)S(1)} %get-tuple-element.8, bf16[5120,896]{1,0:T(8,128)(2,1)} %param.11), kind=kOutput, calls=%fused_computation.19 | convolution fusion | flops 18790481920 | bytes 54788096 | tf_op jit(solution)/shard_map/dot_general | solution.py:16
  68.7 0.0 copy-done
  68.7 35.2 %add_convert_fusion = bf16[2048,5120]{1,0:T(8,128)(2,1)} fusion(f32[2048,5120]{1,0:T(8,128)} %fusion.9, bf16[5120,896]{1,0:T(8,128)(2,1)} %param.12, f32[2048,896]{1,0:T(8,128)} %get-tuple-element.9, bf16[2048,896]{1,0:T(8,128)(2,1)} %param.9), kind=kOutput, calls=%fused_computation | convolution fusion | flops 18824298496 | bytes 83099648 | tf_op jit(solution)/shard_map/dot_general | solution.py:16
  103.8 0.0 all-reduce.2.cloned.1.call-update
  103.9 25.1 %convert_bitcast_fusion.1 = bf16[5120,896]{0,1:T(8,128)(2,1)} fusion(bf16[2048,896]{1,0:T(8,128)(2,1)} %copy-done, bf16[2048,5120]{1,0:T(8,128)(2,1)} %param.7), kind=kOutput, calls=%fused_computation.6 | convolution fusion | flops 18795069440 | bytes 33816576 | tf_op jit(solution)/shard_map/dot_general | solution.py:18
  128.9 12.7 %copy.11 = bf16[5120,896]{1,0:T(8,128)(2,1)} copy(bf16[5120,896]{0,1:T(8,128)(2,1)} %convert_bitcast_fusion.1) | data formatting | bytes 18350080
  141.6 30.0 %convert_bitcast_fusion = bf16[5120,896]{0,1:T(8,128)(2,1)} fusion(bf16[2048,5120]{1,0:T(8,128)(2,1)} %param.7, f32[2048,896]{1,0:T(8,128)} %get-tuple-element.9, bf16[2048,896]{1,0:T(8,128)(2,1)} %param.9), kind=kOutput, calls=%fused_computation.5 | convolution fusion | flops 18807914496 | bytes 41156608 | tf_op jit(solution)/shard_map/dot_general | solution.py:19
  171.6 12.7 %copy.12 = bf16[5120,896]{1,0:T(8,128)(2,1)} copy(bf16[5120,896]{0,1:T(8,128)(2,1)} %convert_bitcast_fusion) | data formatting | bytes 18350080
  184.3 29.6 %convolution_convert_fusion = bf16[896,5120]{1,0:T(8,128)(2,1)} fusion(bf16[2048,5120]{1,0:T(8,128)(2,1)} %param.8, bf16[2048,896]{1,0:T(8,128)(2,1)} %param.10, bf16[2048,896]{1,0:T(8,128)(2,1)} %param.9), kind=kOutput, calls=%fused_computation.9 | convolution fusion | flops 18809749504 | bytes 37486592 | tf_op jit(solution)/shard_map/dot_general | solution.py:20
  213.9 254.7 %all-reduce.2.cloned.1.call-done = bf16[2048,5120]{1,0:T(8,128)(2,1)} async-done(((bf16[2048,5120]{1,0:T(8,128)(2,1)}), bf16[2048,5120]{1,0:T(8,128)(2,1)}) %all-reduce.2.cloned.1.call-update) | async-done | bytes 20971536 | tf_op jit(solution)/shard_map/psum | solution.py:17
  468.6 17.3 %copy.14 = bf16[2048,5120]{1,0:T(8,128)(2,1)} copy(bf16[2048,5120]{1,0:T(8,128)(2,1)} %all-reduce.2.cloned.1.call-done) | data formatting | bytes 41943040
Async XLA Ops:
  7.2 461.5 %all-reduce.2.cloned.1.call-start = ((), (), s32[]{:S(2)}) async-start(), calls=%async_computation | async-start | bytes 41943040 | tf_op jit(solution)/shard_map/psum | solution.py:17
  38.6 30.0 %copy-start = (bf16[2048,896]{1,0:T(8,128)(2,1)}, bf16[2048,896]{1,0:T(8,128)(2,1)S(1)}, u32[]{:S(2)}) copy-start(bf16[2048,896]{1,0:T(8,128)(2,1)S(1)} %get-tuple-element.8) | copy-start | bytes 11010052
Sparse Core Ops, SparseCore 0:
  104.0 364.6 all-reduce.1
where the time goes:
time: 494 us; the launch traced here: 493 us
  waiting for transfers between devices  255 us (52%)
  matrix products  181 us (37%)
  local copies, waits for them, and re-layouts  42.7 us (9%)
  between operations  14 us (3%)
    psum x1, waiting for transfers between devices, step(): dx = lax.psum(term.astype(jnp.bfloat16), 'tp')  255 us
    unnamed x5, local copies, waits for them, and re-layouts  42.7 us
    dot_general x1, matrix products, step(): jnp.dot(d_up, w_up.T, preferred_element_type=jnp.float32)  35.2 us
    dot_general x1, matrix products, step(): d_hidden = jnp.dot(dy, w_down.T, preferred_element_type=jnp.float32)  31.4 us
    dot_general x1, matrix products, step(): dw_up = jnp.dot(x.T, d_up, preferred_element_type=jnp.float32)  30 us
    dot_general x1, matrix products, step(): jnp.dot(d_gate, w_gate.T, preferred_element_type=jnp.float32)  30 us
    dot_general x1, matrix products, step(): jnp.dot(hidden.astype(jnp.bfloat16).T, dy, preferred_element_type=jnp.flo...  29.6 us
    dot_general x1, matrix products, step(): dw_gate = jnp.dot(x.T, d_gate, preferred_element_type=jnp.float32)  25.1 us
  transfers between devices with their start and end apart: 1, of which 1 were waited for; matrix products, arithmetic and copies ran while one was open for 22% of the time, Pallas kernels for 0%

commit v1 on v0

v1 whole, which is shorter than its diff:
```python
import jax
import jax.numpy as jnp
from jax import lax
from jax.experimental import pallas as pl
from jax.experimental.pallas import tpu as pltpu
from jax.sharding import PartitionSpec as P

MESH = pl.DeviceIdType.MESH
bf, f32 = jnp.bfloat16, jnp.float32
DMA = pltpu.SemaphoreType.DMA
L = 128

T_ROWS, D_MODEL, FF = 2048, 5120, 896
HC = D_MODEL // 2
A, A2, BO, BT, MC = 6 * L, 3 * L, 12 * L, 2 * L, 14 * L

R, D = 32, 2
NB = T_ROWS // R
NS, NR, W = 2 * D, 8 * D, 2
STEPS = NB + 8 * D
FILL, DRAIN = 4 * D, NB + 3 * D

G = 256
NG, BPG, PPG = T_ROWS // G, G // R, 6
LEAD = PPG
Q = D_MODEL // 4
F0 = 512
XT, YT = 256, 512
NX, NY = D_MODEL // XT, D_MODEL // YT
P2 = NG * PPG
PIECES2 = NX + NY


def dot(a, b, ca, cb):
    return lax.dot_general(a, b, (((ca,), (cb,)), ((), ())), preferred_element_type=f32)


SCRATCH = dict(
    WD=pltpu.VMEM((FF, D_MODEL), bf),
    WGU=pltpu.VMEM((D_MODEL, 2 * FF), bf),
    DGU=pltpu.VMEM((T_ROWS, 2 * FF), bf),
    HID=pltpu.VMEM((T_ROWS, FF), bf),
    DY=pltpu.VMEM((2, G, D_MODEL), bf),
    GA=pltpu.VMEM((2, G, FF), bf),
    UP=pltpu.VMEM((2, G, FF), bf),
    PST=pltpu.VMEM((2, G, Q), bf),
    OST=pltpu.VMEM((2, G, Q), f32),
    H=pltpu.VMEM((NR, R, HC), f32),
    PT=pltpu.VMEM((4, R, HC), bf),
    F=pltpu.VMEM((NR, R, HC), bf),
    SR=pltpu.VMEM((NS, R, MC), bf),
    SL=pltpu.VMEM((NS, R, MC), bf),
    SY=pltpu.VMEM((NS, R, MC), bf),
    RR=pltpu.VMEM((NS, R, MC), bf),
    RL=pltpu.VMEM((NS, R, MC), bf),
    RY=pltpu.VMEM((NS, R, MC), bf),
    ss=DMA((3, NS)),
    rs=DMA((3, NS)),
    lh=DMA((4,)),
    lp=DMA((4,)),
    os=DMA((4,)),
    ds=DMA((4,)),
    dr=DMA((4,)),
    wd=DMA((1,)),
    wgu=DMA((4, 2)),
    ld=DMA((2, 3)),
    ps=DMA((2,)),
    pr=DMA((NG, 2)),
    ow=DMA((2,)),
    xl=DMA((2,)),
    yl=DMA((2,)),
    xo=DMA((2, 2)),
    yo=DMA((2,)),
)


OPERANDS = ("x", "dy", "gate", "up", "wg", "wu", "wd_h", "dx", "dwg", "dwu", "dwd", "own", "pt")


class Kernel:
    def __init__(s, *refs):
        s.__dict__.update(zip(OPERANDS + tuple(SCRATCH), refs, strict=True))
        i = lax.axis_index("tp")
        s.y, s.z, s.c = i // 8, lax.rem(i // 2, 4), lax.rem(i, 2)
        s.zm = 3 - s.z
        s.yid, s.cid = i + 8 - 16 * s.y, i + 1 - 2 * s.c
        s.rid, s.lid = jnp.minimum(i + 2, 15), jnp.maximum(i - 2, 0)
        s.has_r, s.has_l = s.z < 3, s.z > 0
        m = pl.multiple_of
        s.a0, s.o0 = m(s.y * A, L), m((1 - s.y) * A, L)
        s.a3, s.o3 = m(s.a0 + A2, L), m(s.o0 + A2, L)
        bz = BO + s.z * BT
        s.b_own, s.b_oth = m(bz + s.y * L, L), m(bz + (1 - s.y) * L, L)
        s.half = m(s.c * HC, HC)

    def barrier(s):
        b = pltpu.get_barrier_semaphore()

        def greet(d):
            pl.semaphore_signal(b, inc=1, device_id={"tp": d}, device_id_type=MESH)

        greet(s.yid)
        greet(s.cid)
        pl.when(s.has_r)(lambda: greet(s.rid))
        pl.when(s.has_l)(lambda: greet(s.lid))
        both = s.has_r & s.has_l
        pl.when(both)(lambda: pl.semaphore_wait(b, 4))
        pl.when(jnp.logical_not(both))(lambda: pl.semaphore_wait(b, 3))


    def loads(s, b):
        rows = pl.ds(pl.multiple_of(b * R, R), R)
        k = lax.rem(b, 4)
        return (
            pltpu.make_async_copy(s.own.at[rows], s.H.at[lax.rem(b, NR)], s.lh.at[k]),
            pltpu.make_async_copy(s.pt.at[rows], s.PT.at[k], s.lp.at[k]),
        )

    def start_loads(s, b):
        for c in s.loads(b):
            c.start()

    def message(s, link, t, kind):
        k = lax.rem(t, NS)
        lo, hi = (
            ((5 * L, MC), (0, 9 * L), (0, 7 * L)),
            ((0, MC),) * 3,
            ((0, 9 * L), (5 * L, MC), (7 * L, MC)),
        )[kind][link]
        src, dst = ((s.SR, s.RR), (s.SL, s.RL), (s.SY, s.RY))[link]
        at = (k, slice(None), pl.ds(lo, hi - lo))
        return pltpu.make_async_remote_copy(
            src_ref=src.at[at],
            dst_ref=dst.at[at],
            send_sem=s.ss.at[link, k],
            recv_sem=s.rs.at[link, k],
            device_id={"tp": (s.rid, s.lid, s.yid)[link]},
            device_id_type=MESH,
        )

    def messages(s, t, valid, do, right, left):
        def kind(k):
            do(s.message(2, t, k))
            pl.when(right)(lambda: do(s.message(0, t, k)))
            pl.when(left)(lambda: do(s.message(1, t, k)))

        pl.when(valid & (t < FILL))(lambda: kind(0))
        pl.when(valid & (t >= FILL) & (t < DRAIN))(lambda: kind(1))
        pl.when(valid & (t >= DRAIN) & (t < STEPS - D))(lambda: kind(2))

    def outs(s, b):
        k, q = lax.rem(b, NR), lax.rem(b, 4)
        dst = s.dx.at[pl.ds(pl.multiple_of(b * R, R), R), pl.ds(s.half, HC)]
        return (
            pltpu.make_async_copy(s.F.at[k], dst, s.os.at[q]),
            pltpu.make_async_remote_copy(
                src_ref=s.F.at[k],
                dst_ref=dst,
                send_sem=s.ds.at[q],
                recv_sem=s.dr.at[q],
                device_id={"tp": s.cid},
                device_id_type=MESH,
            ),
        )

    def wait_outs(s, b):
        for c in s.outs(b):
            c.wait()

    def service(s, t):
        s.messages(t - D, t >= D, lambda c: c.wait_recv(), s.has_l, s.has_r)
        s.messages(t - NS, t >= NS, lambda c: c.wait_send(), s.has_r, s.has_l)

        @pl.when(t < NB)
        def _():
            for c in s.loads(t):
                c.wait()

        @pl.when(t + 2 < NB)
        def _():
            g = (t + 2) // BPG
            pl.when(lax.rem(t + 2, BPG) == 0)(lambda: s.wait_partner(g))
            s.start_loads(t + 2)

        pl.when(t >= 8 * D + W)(lambda: s.wait_outs(t - 8 * D - W))

        def h(o):
            return lax.rem(t - o + 4 * NR, NR)

        H, F, z, zm = s.H, s.F, s.z, s.zm
        k, kr = lax.rem(t, NS), lax.rem(t + NS - D, NS)
        RY, RR, RL = s.RY.at[kr], s.RR.at[kr], s.RL.at[kr]
        SY, SR, SL = s.SY.at[k], s.SR.at[k], s.SL.at[k]

        H[h(0)] = H[h(0)] + s.PT[lax.rem(t, 4)].astype(f32)
        own = (h(D), slice(None), pl.ds(s.a0, A))
        H[own] = H[own] + RY[:, 0 : 6 * L].astype(f32)
        rooted = (h(4 * D), slice(None), pl.ds(s.b_own, L))
        F[rooted] = (H[rooted] + RY[:, 6 * L : 7 * L].astype(f32)).astype(bf)
        F[h(5 * D), :, pl.ds(s.b_oth, L)] = RY[:, 7 * L : 8 * L]
        F[h(5 * D + D * z), :, pl.ds(s.o0, A2)] = RY[:, 8 * L : 11 * L]
        F[h(5 * D + D * zm), :, pl.ds(s.o3, A2)] = RY[:, 11 * L : 14 * L]
        to_r = jnp.where(s.has_l, RR[:, 11 * L :].astype(f32), 0.0) + H[h(D + D * z), :, pl.ds(s.a3, A2)]
        to_l = jnp.where(s.has_r, RL[:, : 3 * L].astype(f32), 0.0) + H[h(D + D * zm), :, pl.ds(s.a0, A2)]
        to_r, to_l = to_r.astype(bf), to_l.astype(bf)
        f3 = jnp.where(s.has_r, RL[:, 11 * L :], to_r)
        f0 = jnp.where(s.has_l, RR[:, : 3 * L], to_l)
        F[h(4 * D + D * zm), :, pl.ds(s.a3, A2)] = f3
        F[h(4 * D + D * z), :, pl.ds(s.a0, A2)] = f0
        SR[:, 11 * L :], SR[:, : 3 * L] = to_r, f0
        SL[:, : 3 * L], SL[:, 11 * L :] = to_l, f3
        SY[:, 8 * L : 11 * L], SY[:, 11 * L :] = f0, f3
        hr, hl = h(D * z), h(D * zm)
        for q in range(4):
            b = pl.ds(BO + q * BT, BT)
            m = pl.ds(3 * L + q * BT, BT)
            rr, rl = RR[:, m], RL[:, m]
            sum_r = H[hr, :, b] + jnp.where(s.has_l, rr.astype(f32), 0.0)

            @pl.when(z == q)
            def _():
                H[hr, :, b] = sum_r

            sum_l = H[hl, :, b] + jnp.where(s.has_r, rl.astype(f32), 0.0)

            @pl.when(z == q)
            def _():
                H[hl, :, b] = sum_l

            fq = h(5 * D + D * jnp.abs(z - q))

            @pl.when(z > q)
            def _():
                F[fq, :, b] = rr

            @pl.when(z < q)
            def _():
                F[fq, :, b] = rl

            done = F[fq, :, b]
            SR[:, m] = jnp.where(z >= q, done, sum_r.astype(bf))
            SL[:, m] = jnp.where(z <= q, done, sum_l.astype(bf))
        SY[:, : 6 * L] = H[h(0), :, pl.ds(s.o0, A)].astype(bf)
        SY[:, 6 * L : 7 * L] = H[h(3 * D), :, pl.ds(s.b_oth, L)].astype(bf)
        SY[:, 7 * L : 8 * L] = F[h(4 * D), :, pl.ds(s.b_own, L)]
        s.messages(t, t >= 0, lambda c: c.start(), s.has_r, s.has_l)

        @pl.when(t >= 8 * D)
        def _():
            for c in s.outs(t - 8 * D):
                c.start()

    def finish(s):
        for b in range(NB - W, NB):
            s.wait_outs(b)
        for t in range(STEPS - D - NS + D, STEPS - D):
            s.message(2, t, 2).wait_send()
            pl.when(s.has_r)(lambda t=t: s.message(0, t, 2).wait_send())
            pl.when(s.has_l)(lambda t=t: s.message(1, t, 2).wait_send())


    def weights(s):
        def copy(src, dst, sem):
            return pltpu.make_async_copy(src, dst, sem)

        first = copy(s.wd_h, s.WD, s.wd.at[0])
        quarters = []
        for j in range(4):
            rows = pl.ds(s.quarter(j), Q)
            quarters.append(
                [
                    copy(w.at[rows], s.WGU.at[rows, pl.ds(n * FF, FF)], s.wgu.at[j, n])
                    for n, w in enumerate((s.wg, s.wu))
                ]
            )
        return first, quarters

    def quarter(s, j):
        mine = jnp.where(j < 2, 1 - s.c, s.c)
        return pl.multiple_of(mine * HC + lax.rem(j, 2) * Q, Q)

    def group_loads(s, g):
        k = lax.rem(g, 2)
        rows = pl.ds(pl.multiple_of(g * G, G), G)
        return [
            pltpu.make_async_copy(a.at[rows], v.at[k], s.ld.at[k, n])
            for n, (a, v) in enumerate(((s.dy, s.DY), (s.gate, s.GA), (s.up, s.UP)))
        ]

    def to_partner(s, g, j):
        rows = pl.ds(pl.multiple_of(g * G, G), G)
        return pltpu.make_async_remote_copy(
            src_ref=s.PST.at[j],
            dst_ref=s.pt.at[rows, pl.ds(pl.multiple_of(j * Q, Q), Q)],
            send_sem=s.ps.at[j],
            recv_sem=s.pr.at[g, j],
            device_id={"tp": s.cid},
            device_id_type=MESH,
        )

    def to_own(s, g, j):
        rows = pl.ds(pl.multiple_of(g * G, G), G)
        dst = s.own.at[rows, pl.ds(pl.multiple_of(j * Q, Q), Q)]
        return pltpu.make_async_copy(s.OST.at[j], dst, s.ow.at[j])

    def wait_partner(s, g):
        for j in range(2):
            s.to_partner(g, j).wait_recv()

    def hidden(s, g, lo, hi):
        k = lax.rem(g, 2)
        rows = pl.ds(pl.multiple_of(g * G, G), G)
        d = dot(s.DY[k], s.WD[lo:hi, :], 1, 1)
        a, u = s.GA[k, :, lo:hi].astype(f32), s.UP[k, :, lo:hi].astype(f32)
        sig = jax.nn.sigmoid(a)
        silu = a * sig
        s.DGU[rows, lo:hi] = (d * u * (sig + silu * (1.0 - sig))).astype(bf)
        s.DGU[rows, FF + lo : FF + hi] = (d * silu).astype(bf)
        s.HID[rows, lo:hi] = (silu * u).astype(bf)

    def term(s, g, j):
        rows = pl.ds(pl.multiple_of(g * G, G), G)
        return dot(s.DGU[rows, :], s.WGU[pl.ds(s.quarter(j), Q), :], 1, 1)

    def before1(s, u):
        g = u // PPG

        @pl.when(u > 0)
        def _():
            for j in range(2):
                s.to_partner(g - 1, j).wait_send()
                s.to_own(g - 1, j).wait()

        @pl.when(u == LEAD)
        def _():
            s.wait_partner(0)
            s.start_loads(0)
            s.start_loads(1)

        @pl.when(g + 1 < NG)
        def _():
            for c in s.group_loads(g + 1):
                c.start()

    def piece1(s, u):
        g, r = u // PPG, lax.rem(u, PPG)
        first, quarters = s.weights()

        @pl.when(r == 0)
        def _():
            for c in s.group_loads(g):
                c.wait()
            pl.when(g == 0)(lambda: first.wait())
            s.hidden(g, 0, F0)

        pl.when(r == 1)(lambda: s.hidden(g, F0, FF))
        for j in range(4):

            @pl.when(u == 2 + j)
            def _(j=j):
                for c in quarters[j]:
                    c.wait()

        @pl.when((r == 2) | (r == 3))
        def _():
            j = r - 2
            s.PST[j] = s.term(g, r - 2).astype(bf)
            s.to_partner(g, j).start()

        @pl.when(r >= 4)
        def _():
            j = r - 4
            s.OST[j] = s.term(g, r - 2)
            s.to_own(g, j).start()


    def x_tile(s, q):
        k = lax.rem(q, 2)
        v = s.WGU.at[pl.ds(0, T_ROWS), pl.ds(pl.multiple_of(k * XT, XT), XT)]
        src = s.x.at[:, pl.ds(pl.multiple_of(q * XT, XT), XT)]
        return v, pltpu.make_async_copy(src, v, s.xl.at[k])

    def y_tile(s, q):
        k = lax.rem(q, 2)
        v = s.WGU.at[pl.ds(T_ROWS, T_ROWS), pl.ds(pl.multiple_of(k * YT, YT), YT)]
        src = s.dy.at[:, pl.ds(pl.multiple_of(q * YT, YT), YT)]
        return v, pltpu.make_async_copy(src, v, s.yl.at[k])

    def x_out(s, q):
        k = lax.rem(q, 2)
        v = s.WGU.at[pl.ds(pl.multiple_of(2 * T_ROWS + k * XT, XT), XT), :]
        rows = pl.ds(pl.multiple_of(q * XT, XT), XT)
        return v, [
            pltpu.make_async_copy(v.at[:, pl.ds(n * FF, FF)], o.at[rows], s.xo.at[k, n])
            for n, o in enumerate((s.dwg, s.dwu))
        ]

    def y_out(s, q):
        k = lax.rem(q, 2)
        v = s.WGU.at[pl.ds(0, FF), pl.ds(pl.multiple_of(2 * XT + k * YT, YT), YT)]
        dst = s.dwd.at[:, pl.ds(pl.multiple_of(q * YT, YT), YT)]
        return v, pltpu.make_async_copy(v, dst, s.yo.at[k])

    def piece2(s, u):
        m = u - P2
        r = lax.rem(m, 3)

        @pl.when(m == 0)
        def _():
            s.x_tile(0)[1].start()
            s.y_tile(0)[1].start()

        @pl.when(r < 2)
        def _():
            q = (m // 3) * 2 + r
            pl.when(q + 1 < NX)(lambda: s.x_tile(q + 1)[1].start())
            tile, load = s.x_tile(q)
            load.wait()
            out, stores = s.x_out(q)

            @pl.when(q >= 2)
            def _():
                for c in s.x_out(q - 2)[1]:
                    c.wait()

            out[...] = dot(tile[...], s.DGU[...], 0, 0).astype(bf)
            for c in stores:
                c.start()

        @pl.when(r == 2)
        def _():
            q = m // 3
            pl.when(q + 1 < NY)(lambda: s.y_tile(q + 1)[1].start())
            tile, load = s.y_tile(q)
            load.wait()
            out, store = s.y_out(q)
            pl.when(q >= 2)(lambda: s.y_out(q - 2)[1].wait())
            out[...] = dot(s.HID[...], tile[...], 0, 0).astype(bf)
            store.start()

    def run(s):
        for c in s.group_loads(0):
            c.start()
        first, quarters = s.weights()
        first.start()
        for j in range(4):
            for c in quarters[j]:
                c.start()
        s.barrier()

        def iteration(u, _):
            pl.when((u <= P2) & (lax.rem(u, PPG) == 0))(lambda: s.before1(u))
            pl.when(u >= LEAD)(lambda: s.service(u - LEAD))
            pl.when(u < P2)(lambda: s.piece1(u))
            pl.when((u >= P2) & (u < P2 + PIECES2))(lambda: s.piece2(u))
            return 0

        lax.fori_loop(0, LEAD + STEPS, iteration, 0)
        s.finish()
        for q in (NX - 2, NX - 1):
            for c in s.x_out(q)[1]:
                c.wait()
        for q in (NY - 2, NY - 1):
            s.y_out(q)[1].wait()


def solution(mesh):
    def step(x, dy, gate, up, w_gate, w_up, w_down):
        shape = jax.ShapeDtypeStruct
        anywhere = pl.BlockSpec(memory_space=pl.ANY)
        dx, dw_gate, dw_up, dw_down, _, _ = pl.pallas_call(
            lambda *refs: Kernel(*refs).run(),
            out_shape=[
                shape((T_ROWS, D_MODEL), bf),
                shape((D_MODEL, FF), bf),
                shape((D_MODEL, FF), bf),
                shape((FF, D_MODEL), bf),
                shape((T_ROWS, HC), f32),
                shape((T_ROWS, HC), bf),
            ],
            in_specs=[anywhere] * 7,
            out_specs=[anywhere] * 6,
            scratch_shapes=list(SCRATCH.values()),
            compiler_params=pltpu.CompilerParams(
                collective_id=0, has_side_effects=True, vmem_limit_bytes=67043328
            ),
            name="mlp_backward",
        )(x, dy, gate, up, w_gate, w_up, w_down)
        return dx, dw_gate, dw_up, dw_down

    tokens, columns, rows = P("dp", None), P(None, "tp"), P("tp", None)
    return jax.shard_map(
        step,
        mesh=mesh,
        in_specs=(tokens, tokens, P("dp", "tp"), P("dp", "tp"), columns, columns, rows),
        out_specs=(tokens, P("dp", "tp"), P("dp", "tp"), P(("dp", "tp"), None)),
        check_vma=False,
    )
```

time: 494 us -> 262 us (0.53)
  waiting for transfers between devices: 255 us -> 0 us
  Pallas kernels: 0 us -> 220 us
  matrix products: 181 us -> 0 us
  between operations: 14 us -> 0.64 us
    psum x1 -> x0, waiting for transfers between devices: 255 us -> none  [step(): dx = lax.psum(term.astype(jnp.bfloat16), 'tp')]
    pallas_call x0 -> x1, Pallas kernels: none -> 220 us  [step(): pl.pallas_call(lambda *refs: Kernel(*refs).run(), out_shape=[shape((T_ROW...]
    dot_general x6 -> x0, matrix products: 181 us -> none  [the longest x1 35.2 us: step(): jnp.dot(d_up, w_up.T, preferred_element_type=jnp.float32)]
    unnamed x5 -> x4, local copies, waits for them, and re-layouts: 42.7 us -> 41.2 us
  transfers between devices with their start and end apart: 1 -> 0, of which waited for: 1 -> 0; matrix products, arithmetic and copies ran while one was open for 22% -> 0% of each run, Pallas kernels for 0% -> 0%
where the time goes in v1:
time: 262 us; the launch traced here: 261 us
  Pallas kernels  220 us (84%)
  local copies, waits for them, and re-layouts  41.2 us (16%)
    pallas_call x1, Pallas kernels, step(): pl.pallas_call(lambda *refs: Kernel(*refs).run(), out_shape=[shape((T_ROW...  220 us
    unnamed x4, local copies, waits for them, and re-layouts  41.2 us

profile of v1, /device:TPU:0, one launch (start us, length us, event | category | flops | bytes accessed | tf_op | source)
XLA Modules:
  0.0 261.4 jit_solution(15103043997947045424)
XLA Ops:
  0.6 219.6 %mlp_backward.1 = (bf16[2048,5120]{1,0:T(8,128)(2,1)}, bf16[5120,896]{1,0:T(8,128)(2,1)}, bf16[5120,896]{1,0:T(8,128)(2,1)}, bf16[896,5120]{1,0:T(8,128)(2,1)}, ...) custom-call(bf16[2048,5120]{1,0:T(8,128)(2,1)} %refs_0_.1, bf16[2048,5120]{1,0:T(8,128)(2,1)} %refs_1_.1, ...), custom_call_target="tpu_custom_call" | custom-call | tf_op jit(solution)/shard_map/mlp_backward/pallas_call | solution.py:471
  220.2 17.3 %copy.15 = bf16[2048,5120]{1,0:T(8,128)(2,1)} copy(bf16[2048,5120]{1,0:T(8,128)(2,1)} %get-tuple-element.16) | data formatting | bytes 41943040
  237.5 8.0 %copy.16 = bf16[5120,896]{1,0:T(8,128)(2,1)} copy(bf16[5120,896]{1,0:T(8,128)(2,1)} %get-tuple-element.17) | data formatting | bytes 18350080
  245.5 8.0 %copy.17 = bf16[5120,896]{1,0:T(8,128)(2,1)} copy(bf16[5120,896]{1,0:T(8,128)(2,1)} %get-tuple-element.18) | data formatting | bytes 18350080
  253.5 7.9 %copy.18 = bf16[896,5120]{1,0:T(8,128)(2,1)} copy(bf16[896,5120]{1,0:T(8,128)(2,1)} %get-tuple-element.19) | data formatting | bytes 18350080

commit v2 on v1

--- a/solution.py
+++ b/solution.py
@@ -16,19 +16,22 @@
 
 R, D = 32, 2
 NB = T_ROWS // R
-NS, NR, W = 2 * D, 8 * D, 2
+NS, NR, NH, W = 2 * D, 16, 4 * D + 4, 2
 STEPS = NB + 8 * D
 FILL, DRAIN = 4 * D, NB + 3 * D
 
 G = 256
 NG, BPG, PPG = T_ROWS // G, G // R, 6
 LEAD = PPG
+AHEAD = 2
+DIRECT = 4
 Q = D_MODEL // 4
 F0 = 512
 XT, YT = 256, 512
 NX, NY = D_MODEL // XT, D_MODEL // YT
 P2 = NG * PPG
-PIECES2 = NX + NY
+WIDE = 4
+PIECES2 = NX + 2 * NY - WIDE
 
 
 def dot(a, b, ca, cb):
@@ -36,16 +39,14 @@
 
 
 SCRATCH = dict(
-    WD=pltpu.VMEM((FF, D_MODEL), bf),
-    WGU=pltpu.VMEM((D_MODEL, 2 * FF), bf),
     DGU=pltpu.VMEM((T_ROWS, 2 * FF), bf),
     HID=pltpu.VMEM((T_ROWS, FF), bf),
-    DY=pltpu.VMEM((2, G, D_MODEL), bf),
+    POOL=pltpu.VMEM((T_ROWS, 2 * (XT + YT)), bf),
     GA=pltpu.VMEM((2, G, FF), bf),
     UP=pltpu.VMEM((2, G, FF), bf),
     PST=pltpu.VMEM((2, G, Q), bf),
     OST=pltpu.VMEM((2, G, Q), f32),
-    H=pltpu.VMEM((NR, R, HC), f32),
+    H=pltpu.VMEM((NH, R, HC), f32),
     PT=pltpu.VMEM((4, R, HC), bf),
     F=pltpu.VMEM((NR, R, HC), bf),
     SR=pltpu.VMEM((NS, R, MC), bf),
@@ -58,23 +59,21 @@
     rs=DMA((3, NS)),
     lh=DMA((4,)),
     lp=DMA((4,)),
-    os=DMA((4,)),
-    ds=DMA((4,)),
-    dr=DMA((4,)),
-    wd=DMA((1,)),
+    os=DMA((8,)),
+    ds=DMA((8,)),
+    dr=DMA((8,)),
+    wd=DMA((4,)),
     wgu=DMA((4, 2)),
-    ld=DMA((2, 3)),
+    ld=DMA((2, 6)),
     ps=DMA((2,)),
     pr=DMA((NG, 2)),
     ow=DMA((2,)),
     xl=DMA((2,)),
     yl=DMA((2,)),
-    xo=DMA((2, 2)),
-    yo=DMA((2,)),
 )
 
 
-OPERANDS = ("x", "dy", "gate", "up", "wg", "wu", "wd_h", "dx", "dwg", "dwu", "dwd", "own", "pt")
+OPERANDS = ("x", "dy", "gate", "up", "wg", "wu", "wd_h", "dx", "WGU", "WD", "own", "pt")
 
 
 class Kernel:
@@ -112,13 +111,9 @@
         rows = pl.ds(pl.multiple_of(b * R, R), R)
         k = lax.rem(b, 4)
         return (
-            pltpu.make_async_copy(s.own.at[rows], s.H.at[lax.rem(b, NR)], s.lh.at[k]),
+            pltpu.make_async_copy(s.own.at[rows], s.H.at[lax.rem(b, NH)], s.lh.at[k]),
             pltpu.make_async_copy(s.pt.at[rows], s.PT.at[k], s.lp.at[k]),
         )
-
-    def start_loads(s, b):
-        for c in s.loads(b):
-            c.start()
 
     def message(s, link, t, kind):
         k = lax.rem(t, NS)
@@ -149,7 +144,7 @@
         pl.when(valid & (t >= DRAIN) & (t < STEPS - D))(lambda: kind(2))
 
     def outs(s, b):
-        k, q = lax.rem(b, NR), lax.rem(b, 4)
+        k, q = lax.rem(b, NR), lax.rem(b, 8)
         dst = s.dx.at[pl.ds(pl.multiple_of(b * R, R), R), pl.ds(s.half, HC)]
         return (
             pltpu.make_async_copy(s.F.at[k], dst, s.os.at[q]),
@@ -167,46 +162,42 @@
         for c in s.outs(b):
             c.wait()
 
+    def chip_sum(s, b):
+        own, partner = s.loads(b)
+        pl.when(b >= DIRECT)(lambda: own.wait())
+        partner.wait()
+        k = lax.rem(b, NH)
+        s.H[k] = s.H[k] + s.PT[lax.rem(b, 4)].astype(f32)
+
     def service(s, t):
         s.messages(t - D, t >= D, lambda c: c.wait_recv(), s.has_l, s.has_r)
         s.messages(t - NS, t >= NS, lambda c: c.wait_send(), s.has_r, s.has_l)
 
-        @pl.when(t < NB)
-        def _():
-            for c in s.loads(t):
-                c.wait()
-
-        @pl.when(t + 2 < NB)
-        def _():
-            g = (t + 2) // BPG
-            pl.when(lax.rem(t + 2, BPG) == 0)(lambda: s.wait_partner(g))
-            s.start_loads(t + 2)
-
-        pl.when(t >= 8 * D + W)(lambda: s.wait_outs(t - 8 * D - W))
+        def f(o):
+            return lax.rem(t - o + 4 * NR, NR)
 
         def h(o):
-            return lax.rem(t - o + 4 * NR, NR)
+            return lax.rem(t - o + 4 * NH, NH)
 
         H, F, z, zm = s.H, s.F, s.z, s.zm
         k, kr = lax.rem(t, NS), lax.rem(t + NS - D, NS)
         RY, RR, RL = s.RY.at[kr], s.RR.at[kr], s.RL.at[kr]
         SY, SR, SL = s.SY.at[k], s.SR.at[k], s.SL.at[k]
 
-        H[h(0)] = H[h(0)] + s.PT[lax.rem(t, 4)].astype(f32)
         own = (h(D), slice(None), pl.ds(s.a0, A))
         H[own] = H[own] + RY[:, 0 : 6 * L].astype(f32)
-        rooted = (h(4 * D), slice(None), pl.ds(s.b_own, L))
-        F[rooted] = (H[rooted] + RY[:, 6 * L : 7 * L].astype(f32)).astype(bf)
-        F[h(5 * D), :, pl.ds(s.b_oth, L)] = RY[:, 7 * L : 8 * L]
-        F[h(5 * D + D * z), :, pl.ds(s.o0, A2)] = RY[:, 8 * L : 11 * L]
-        F[h(5 * D + D * zm), :, pl.ds(s.o3, A2)] = RY[:, 11 * L : 14 * L]
+        rooted = H[h(4 * D), :, pl.ds(s.b_own, L)] + RY[:, 6 * L : 7 * L].astype(f32)
+        F[f(4 * D), :, pl.ds(s.b_own, L)] = rooted.astype(bf)
+        F[f(5 * D), :, pl.ds(s.b_oth, L)] = RY[:, 7 * L : 8 * L]
+        F[f(5 * D + D * z), :, pl.ds(s.o0, A2)] = RY[:, 8 * L : 11 * L]
+        F[f(5 * D + D * zm), :, pl.ds(s.o3, A2)] = RY[:, 11 * L : 14 * L]
         to_r = jnp.where(s.has_l, RR[:, 11 * L :].astype(f32), 0.0) + H[h(D + D * z), :, pl.ds(s.a3, A2)]
         to_l = jnp.where(s.has_r, RL[:, : 3 * L].astype(f32), 0.0) + H[h(D + D * zm), :, pl.ds(s.a0, A2)]
         to_r, to_l = to_r.astype(bf), to_l.astype(bf)
         f3 = jnp.where(s.has_r, RL[:, 11 * L :], to_r)
         f0 = jnp.where(s.has_l, RR[:, : 3 * L], to_l)
-        F[h(4 * D + D * zm), :, pl.ds(s.a3, A2)] = f3
-        F[h(4 * D + D * z), :, pl.ds(s.a0, A2)] = f0
+        F[f(4 * D + D * zm), :, pl.ds(s.a3, A2)] = f3
+        F[f(4 * D + D * z), :, pl.ds(s.a0, A2)] = f0
         SR[:, 11 * L :], SR[:, : 3 * L] = to_r, f0
         SL[:, : 3 * L], SL[:, 11 * L :] = to_l, f3
         SY[:, 8 * L : 11 * L], SY[:, 11 * L :] = f0, f3
@@ -227,7 +218,7 @@
             def _():
                 H[hl, :, b] = sum_l
 
-            fq = h(5 * D + D * jnp.abs(z - q))
+            fq = f(5 * D + D * jnp.abs(z - q))
 
             @pl.when(z > q)
             def _():
@@ -242,13 +233,25 @@
             SL[:, m] = jnp.where(z <= q, done, sum_l.astype(bf))
         SY[:, : 6 * L] = H[h(0), :, pl.ds(s.o0, A)].astype(bf)
         SY[:, 6 * L : 7 * L] = H[h(3 * D), :, pl.ds(s.b_oth, L)].astype(bf)
-        SY[:, 7 * L : 8 * L] = F[h(4 * D), :, pl.ds(s.b_own, L)]
+        SY[:, 7 * L : 8 * L] = F[f(4 * D), :, pl.ds(s.b_own, L)]
         s.messages(t, t >= 0, lambda c: c.start(), s.has_r, s.has_l)
 
         @pl.when(t >= 8 * D)
         def _():
             for c in s.outs(t - 8 * D):
                 c.start()
+
+        pl.when(t >= 8 * D + W)(lambda: s.wait_outs(t - 8 * D - W))
+
+        @pl.when(t + AHEAD < NB)
+        def _():
+            b = t + AHEAD
+            own, partner = s.loads(b)
+            pl.when(lax.rem(b, BPG) == 0)(lambda: s.wait_partner(b // BPG))
+            pl.when(b >= DIRECT)(lambda: own.start())
+            partner.start()
+
+        pl.when(t + 1 < NB)(lambda: s.chip_sum(t + 1))
 
     def finish(s):
         for b in range(NB - W, NB):
@@ -263,8 +266,10 @@
         def copy(src, dst, sem):
             return pltpu.make_async_copy(src, dst, sem)
 
-        first = copy(s.wd_h, s.WD, s.wd.at[0])
-        quarters = []
+        first, quarters = [], []
+        for j in range(4):
+            at = (slice(None), pl.ds(j * Q, Q))
+            first.append(copy(s.wd_h.at[at], s.WD.at[at], s.wd.at[j]))
         for j in range(4):
             rows = pl.ds(s.quarter(j), Q)
             quarters.append(
@@ -279,12 +284,21 @@
         mine = jnp.where(j < 2, 1 - s.c, s.c)
         return pl.multiple_of(mine * HC + lax.rem(j, 2) * Q, Q)
 
+    def dy_part(s, g, j):
+        return pl.ds(pl.multiple_of(lax.rem(g, 2) * 4 * G + j * G, G), G)
+
     def group_loads(s, g):
         k = lax.rem(g, 2)
         rows = pl.ds(pl.multiple_of(g * G, G), G)
-        return [
-            pltpu.make_async_copy(a.at[rows], v.at[k], s.ld.at[k, n])
-            for n, (a, v) in enumerate(((s.dy, s.DY), (s.gate, s.GA), (s.up, s.UP)))
+        parts = [
+            pltpu.make_async_copy(
+                s.dy.at[rows, pl.ds(j * Q, Q)], s.POOL.at[s.dy_part(g, j), pl.ds(0, Q)], s.ld.at[k, j]
+            )
+            for j in range(4)
+        ]
+        return parts + [
+            pltpu.make_async_copy(a.at[rows], v.at[k], s.ld.at[k, 4 + n])
+            for n, (a, v) in enumerate(((s.gate, s.GA), (s.up, s.UP)))
         ]
 
     def to_partner(s, g, j):
@@ -310,7 +324,10 @@
     def hidden(s, g, lo, hi):
         k = lax.rem(g, 2)
         rows = pl.ds(pl.multiple_of(g * G, G), G)
-        d = dot(s.DY[k], s.WD[lo:hi, :], 1, 1)
+        d = sum(
+            dot(s.POOL[s.dy_part(g, j), 0:Q], s.WD[lo:hi, j * Q : (j + 1) * Q], 1, 1)
+            for j in range(4)
+        )
         a, u = s.GA[k, :, lo:hi].astype(f32), s.UP[k, :, lo:hi].astype(f32)
         sig = jax.nn.sigmoid(a)
         silu = a * sig
@@ -323,21 +340,28 @@
         return dot(s.DGU[rows, :], s.WGU[pl.ds(s.quarter(j), Q), :], 1, 1)
 
     def before1(s, u):
-        g = u // PPG
-
-        @pl.when(u > 0)
+        g, r = u // PPG, lax.rem(u, PPG)
+
+        @pl.when(((r == 0) & (u >= 2 * PPG)) | (u == PPG + 2))
         def _():
             for j in range(2):
                 s.to_partner(g - 1, j).wait_send()
                 s.to_own(g - 1, j).wait()
 
+        @pl.when(u == LEAD - 1)
+        def _():
+            s.wait_partner(0)
+            for b in range(AHEAD):
+                s.loads(b)[1].start()
+
         @pl.when(u == LEAD)
         def _():
-            s.wait_partner(0)
-            s.start_loads(0)
-            s.start_loads(1)
-
-        @pl.when(g + 1 < NG)
+            for b in range(DIRECT):
+                for j in range(2):
+                    s.H[b, :, j * Q : (j + 1) * Q] = s.OST[j, b * R : (b + 1) * R, :]
+            s.chip_sum(jnp.int32(0))
+
+        @pl.when((r == 0) & (g + 1 < NG))
         def _():
             for c in s.group_loads(g + 1):
                 c.start()
@@ -348,9 +372,16 @@
 
         @pl.when(r == 0)
         def _():
-            for c in s.group_loads(g):
+            for n, c in enumerate(s.group_loads(g)):
                 c.wait()
-            pl.when(g == 0)(lambda: first.wait())
+                if n < 4:
+
+                    @pl.when(g == 0)
+                    def _(n=n):
+                        first[n].wait()
+                        for c in quarters[n]:
+                            c.start()
+
             s.hidden(g, 0, F0)
 
         pl.when(r == 1)(lambda: s.hidden(g, F0, FF))
@@ -364,7 +395,7 @@
         @pl.when((r == 2) | (r == 3))
         def _():
             j = r - 2
-            s.PST[j] = s.term(g, r - 2).astype(bf)
+            s.PST[j] = s.term(g, j).astype(bf)
             s.to_partner(g, j).start()
 
         @pl.when(r >= 4)
@@ -376,80 +407,70 @@
 
     def x_tile(s, q):
         k = lax.rem(q, 2)
-        v = s.WGU.at[pl.ds(0, T_ROWS), pl.ds(pl.multiple_of(k * XT, XT), XT)]
+        v = s.POOL.at[:, pl.ds(pl.multiple_of(k * XT, XT), XT)]
         src = s.x.at[:, pl.ds(pl.multiple_of(q * XT, XT), XT)]
         return v, pltpu.make_async_copy(src, v, s.xl.at[k])
 
     def y_tile(s, q):
         k = lax.rem(q, 2)
-        v = s.WGU.at[pl.ds(T_ROWS, T_ROWS), pl.ds(pl.multiple_of(k * YT, YT), YT)]
+        v = s.POOL.at[:, pl.ds(pl.multiple_of(2 * XT + k * YT, XT), YT)]
         src = s.dy.at[:, pl.ds(pl.multiple_of(q * YT, YT), YT)]
         return v, pltpu.make_async_copy(src, v, s.yl.at[k])
 
-    def x_out(s, q):
-        k = lax.rem(q, 2)
-        v = s.WGU.at[pl.ds(pl.multiple_of(2 * T_ROWS + k * XT, XT), XT), :]
-        rows = pl.ds(pl.multiple_of(q * XT, XT), XT)
-        return v, [
-            pltpu.make_async_copy(v.at[:, pl.ds(n * FF, FF)], o.at[rows], s.xo.at[k, n])
-            for n, o in enumerate((s.dwg, s.dwu))
-        ]
-
-    def y_out(s, q):
-        k = lax.rem(q, 2)
-        v = s.WGU.at[pl.ds(0, FF), pl.ds(pl.multiple_of(2 * XT + k * YT, YT), YT)]
-        dst = s.dwd.at[:, pl.ds(pl.multiple_of(q * YT, YT), YT)]
-        return v, pltpu.make_async_copy(v, dst, s.yo.at[k])
+    def half_tile(s, q):
+        k, n = lax.rem(q, 2), YT // 2
+        v = s.POOL.at[:, pl.ds(pl.multiple_of(2 * XT + k * YT, XT), n)]
+        src = s.dy.at[:, pl.ds(pl.multiple_of(WIDE * YT + q * n, n), n)]
+        return v, pltpu.make_async_copy(src, v, s.yl.at[k])
 
     def piece2(s, u):
         m = u - P2
-        r = lax.rem(m, 3)
 
         @pl.when(m == 0)
         def _():
             s.x_tile(0)[1].start()
             s.y_tile(0)[1].start()
 
-        @pl.when(r < 2)
-        def _():
-            q = (m // 3) * 2 + r
-            pl.when(q + 1 < NX)(lambda: s.x_tile(q + 1)[1].start())
-            tile, load = s.x_tile(q)
+        @pl.when(m < NX)
+        def _():
+            pl.when(m + 1 < NX)(lambda: s.x_tile(m + 1)[1].start())
+            tile, load = s.x_tile(m)
             load.wait()
-            out, stores = s.x_out(q)
-
-            @pl.when(q >= 2)
-            def _():
-                for c in s.x_out(q - 2)[1]:
-                    c.wait()
-
-            out[...] = dot(tile[...], s.DGU[...], 0, 0).astype(bf)
-            for c in stores:
-                c.start()
-
-        @pl.when(r == 2)
-        def _():
-            q = m // 3
-            pl.when(q + 1 < NY)(lambda: s.y_tile(q + 1)[1].start())
+            rows = pl.ds(pl.multiple_of(m * XT, XT), XT)
+            s.WGU[rows, :] = dot(tile[...], s.DGU[...], 0, 0).astype(bf)
+
+        @pl.when((m >= NX) & (m < NX + WIDE))
+        def _():
+            q = m - NX
+            pl.when(q + 1 < WIDE)(lambda: s.y_tile(q + 1)[1].start())
+            pl.when(q + 1 == WIDE)(lambda: s.half_tile(0)[1].start())
             tile, load = s.y_tile(q)
             load.wait()
-            out, store = s.y_out(q)
-            pl.when(q >= 2)(lambda: s.y_out(q - 2)[1].wait())
-            out[...] = dot(s.HID[...], tile[...], 0, 0).astype(bf)
-            store.start()
+            columns = pl.ds(pl.multiple_of(q * YT, YT), YT)
+            s.WD[:, columns] = dot(s.HID[...], tile[...], 0, 0).astype(bf)
+
+        @pl.when(m >= NX + WIDE)
+        def _():
+            q = m - NX - WIDE
+            pl.when(m + 1 < PIECES2)(lambda: s.half_tile(q + 1)[1].start())
+            tile, load = s.half_tile(q)
+            load.wait()
+            n = YT // 2
+            columns = pl.ds(pl.multiple_of(WIDE * YT + q * n, n), n)
+            s.WD[:, columns] = dot(s.HID[...], tile[...], 0, 0).astype(bf)
 
     def run(s):
-        for c in s.group_loads(0):
-            c.start()
-        first, quarters = s.weights()
-        first.start()
-        for j in range(4):
-            for c in quarters[j]:
-                c.start()
+        first, _ = s.weights()
+        group = s.group_loads(0)
+        for n in range(4):
+            group[n].start()
+            first[n].start()
+        group[4].start()
+        group[5].start()
         s.barrier()
 
         def iteration(u, _):
-            pl.when((u <= P2) & (lax.rem(u, PPG) == 0))(lambda: s.before1(u))
+            pl.when(u <= P2)(lambda: s.before1(u))
             pl.when(u >= LEAD)(lambda: s.service(u - LEAD))
             pl.when(u < P2)(lambda: s.piece1(u))
             pl.when((u >= P2) & (u < P2 + PIECES2))(lambda: s.piece2(u))
@@ -457,36 +478,92 @@
 
         lax.fori_loop(0, LEAD + STEPS, iteration, 0)
         s.finish()
-        for q in (NX - 2, NX - 1):
-            for c in s.x_out(q)[1]:
-                c.wait()
-        for q in (NY - 2, NY - 1):
-            s.y_out(q)[1].wait()
+
+
+XC, WC, YC = 16, 8, 8
+SLOTS, LAG = 6, 2
+
+
+def copy_out(dx, dwgu, dwd, dx_out, dwg_out, dwu_out, dwd_out, mid, rd, wr, gs, us, ys):
+    def part(n, k, j):
+        return pl.ds(j * (n // k), n // k)
+
+    def read(j):
+        at = part(T_ROWS, XC, j)
+        return pltpu.make_async_copy(dx.at[at], mid.at[j % SLOTS], rd.at[j])
+
+    def write(j):
+        at = part(T_ROWS, XC, j)
+        return pltpu.make_async_copy(mid.at[j % SLOTS], dx_out.at[at], wr.at[j])
+
+    rest = []
+    for j in range(WC):
+        at = part(D_MODEL, WC, j)
+        rest.append(pltpu.make_async_copy(dwgu.at[at, pl.ds(0, FF)], dwg_out.at[at], gs.at[j]))
+        rest.append(pltpu.make_async_copy(dwgu.at[at, pl.ds(FF, FF)], dwu_out.at[at], us.at[j]))
+        at = part(FF, YC, j)
+        rest.append(pltpu.make_async_copy(dwd.at[at], dwd_out.at[at], ys.at[j]))
+    for j in range(SLOTS):
+        read(j).start()
+    n = 0
+    for j in range(XC):
+        read(j).wait()
+        write(j).start()
+        for c in rest[n : (j + 1) * len(rest) // XC]:
+            c.start()
+        n = (j + 1) * len(rest) // XC
+        if j >= LAG and j - LAG + SLOTS < XC:
+            write(j - LAG).wait()
+            read(j - LAG + SLOTS).start()
+    for c in rest:
+        c.wait()
+    for j in range(XC - SLOTS, XC):
+        write(j).wait()
 
 
 def solution(mesh):
     def step(x, dy, gate, up, w_gate, w_up, w_down):
         shape = jax.ShapeDtypeStruct
         anywhere = pl.BlockSpec(memory_space=pl.ANY)
-        dx, dw_gate, dw_up, dw_down, _, _ = pl.pallas_call(
+        vmem = pl.BlockSpec(memory_space=pltpu.VMEM)
+        dx, dw_gu, dw_down, _, _ = pl.pallas_call(
             lambda *refs: Kernel(*refs).run(),
+            out_shape=[
+                shape((T_ROWS, D_MODEL), bf),
+                pltpu.VMEM((D_MODEL, 2 * FF), bf),
+                pltpu.VMEM((FF, D_MODEL), bf),
+                shape((T_ROWS, HC), f32),
+                shape((T_ROWS, HC), bf),
+            ],
+            in_specs=[anywhere] * 7,
+            out_specs=[anywhere, vmem, vmem, anywhere, anywhere],
+            scratch_shapes=list(SCRATCH.values()),
+            compiler_params=pltpu.CompilerParams(
+                collective_id=0, has_side_effects=True, vmem_limit_bytes=37 << 20
+            ),
+            name="mlp_backward",
+        )(x, dy, gate, up, w_gate, w_up, w_down)
+        return pl.pallas_call(
+            copy_out,
             out_shape=[
                 shape((T_ROWS, D_MODEL), bf),
                 shape((D_MODEL, FF), bf),
                 shape((D_MODEL, FF), bf),
                 shape((FF, D_MODEL), bf),
-                shape((T_ROWS, HC), f32),
-                shape((T_ROWS, HC), bf),
             ],
-            in_specs=[anywhere] * 7,
-            out_specs=[anywhere] * 6,
-            scratch_shapes=list(SCRATCH.values()),
-            compiler_params=pltpu.CompilerParams(
-                collective_id=0, has_side_effects=True, vmem_limit_bytes=67043328
-            ),
-            name="mlp_backward",
-        )(x, dy, gate, up, w_gate, w_up, w_down)
-        return dx, dw_gate, dw_up, dw_down
+            in_specs=[anywhere, vmem, vmem],
+            out_specs=[anywhere] * 4,
+            scratch_shapes=[
+                pltpu.VMEM((SLOTS, T_ROWS // XC, D_MODEL), bf),
+                DMA((XC,)),
+                DMA((XC,)),
+                DMA((WC,)),
+                DMA((WC,)),
+                DMA((YC,)),
+            ],
+            compiler_params=pltpu.CompilerParams(vmem_limit_bytes=8 << 20),
+            name="copy_out",
+        )(dx, dw_gu, dw_down)
 
     tokens, columns, rows = P("dp", None), P(None, "tp"), P("tp", None)
     return jax.shard_map(

time: 262 us -> 237 us (0.905)
  local copies, waits for them, and re-layouts: 41.2 us -> 0 us
  Pallas kernels: 220 us -> 236 us
    unnamed x4 -> x0, local copies, waits for them, and re-layouts: 41.2 us -> none
    pallas_call x0 -> x1, Pallas kernels: none -> 22.5 us  [step(): pl.pallas_call(copy_out, out_shape=[shape((T_ROWS, D_MODEL), bf), shape((...]
    pallas_call x1, Pallas kernels: 220 us -> 214 us  [step(): pl.pallas_call(lambda *refs: Kernel(*refs).run(), out_shape=[shape((T_ROW...]
where the time goes in v2:
time: 237 us
  Pallas kernels  236 us (100%)
    pallas_call x1, Pallas kernels, step(): pl.pallas_call(lambda *refs: Kernel(*refs).run(), out_shape=[shape((T_ROW...  214 us
    pallas_call x1, Pallas kernels, step(): pl.pallas_call(copy_out, out_shape=[shape((T_ROWS, D_MODEL), bf), shape((...  22.5 us

profile of v2, /device:TPU:0, one launch (start us, length us, event | category | flops | bytes accessed | tf_op | source)
XLA Modules:
  0.0 236.7 jit_solution(13328574535488396927)
XLA Ops:
  0.6 213.5 %mlp_backward.1 = (bf16[2048,5120]{1,0:T(8,128)(2,1)}, bf16[5120,1792]{1,0:T(8,128)(2,1)S(1)}, bf16[896,5120]{1,0:T(8,128)(2,1)S(1)}, f32[2048,2560]{1,0:T(8,128)}, bf16[2048,2560]{1,0:T(8,128)(2,1)}) custom-call(bf16[2048,5120]{1,0:T(8,128)(2,1)} %refs_0_.1, bf16[2048,5120]{1,0:T(8,128)(2,1)} %refs_1_.1, bf16[2048,896]{1,0:T(8,128)(2,1)} %refs_2_.1, ...), custom_call_target="tpu_custom_call" | custom-call | tf_op jit(solution)/shard_map/mlp_backward/pallas_call | solution.py:529
  214.2 22.5 %copy_out.1 = (bf16[2048,5120]{1,0:T(8,128)(2,1)}, bf16[5120,896]{1,0:T(8,128)(2,1)}, bf16[5120,896]{1,0:T(8,128)(2,1)}, bf16[896,5120]{1,0:T(8,128)(2,1)}) custom-call(bf16[2048,5120]{1,0:T(8,128)(2,1)} %get-tuple-element.7.dx, bf16[5120,1792]{1,0:T(8,128)(2,1)S(1)} %get-tuple-element.8.dwgu, bf16[896,5120]{1,0:T(8,128)(2,1)S(1)} %get-tuple-element.9.dwd), custom_call_target="tpu_custom_call" | custom-call | tf_op jit(solution)/shard_map/copy_out/pallas_call | solution.py:546

commit v3 on v2

--- a/solution.py
+++ b/solution.py
@@ -88,8 +88,8 @@
         m = pl.multiple_of
         s.a0, s.o0 = m(s.y * A, L), m((1 - s.y) * A, L)
         s.a3, s.o3 = m(s.a0 + A2, L), m(s.o0 + A2, L)
-        bz = BO + s.z * BT
-        s.b_own, s.b_oth = m(bz + s.y * L, L), m(bz + (1 - s.y) * L, L)
+        s.bz = m(BO + s.z * BT, L)
+        s.b_own, s.b_oth = m(s.bz + s.y * L, L), m(s.bz + (1 - s.y) * L, L)
         s.half = m(s.c * HC, HC)
 
     def barrier(s):
@@ -115,15 +115,14 @@
             pltpu.make_async_copy(s.pt.at[rows], s.PT.at[k], s.lp.at[k]),
         )
 
-    def message(s, link, t, kind):
+    def message(s, link, t, full):
         k = lax.rem(t, NS)
-        lo, hi = (
-            ((5 * L, MC), (0, 9 * L), (0, 7 * L)),
-            ((0, MC),) * 3,
-            ((0, 9 * L), (5 * L, MC), (7 * L, MC)),
-        )[kind][link]
         src, dst = ((s.SR, s.RR), (s.SL, s.RL), (s.SY, s.RY))[link]
-        at = (k, slice(None), pl.ds(lo, hi - lo))
+        at = k
+        if not full:
+            sums, results = ((5 * L, 0), (0, 5 * L), (0, 7 * L))[link]
+            lo = pl.multiple_of(jnp.where(t < FILL, sums, results), L)
+            at = (k, slice(None), pl.ds(lo, (9 * L, 9 * L, 7 * L)[link]))
         return pltpu.make_async_remote_copy(
             src_ref=src.at[at],
             dst_ref=dst.at[at],
@@ -133,15 +132,15 @@
             device_id_type=MESH,
         )
 
-    def messages(s, t, valid, do, right, left):
-        def kind(k):
-            do(s.message(2, t, k))
-            pl.when(right)(lambda: do(s.message(0, t, k)))
-            pl.when(left)(lambda: do(s.message(1, t, k)))
-
-        pl.when(valid & (t < FILL))(lambda: kind(0))
-        pl.when(valid & (t >= FILL) & (t < DRAIN))(lambda: kind(1))
-        pl.when(valid & (t >= DRAIN) & (t < STEPS - D))(lambda: kind(2))
+    def messages(s, t, valid, do, *links):
+        middle = (t >= FILL) & (t < DRAIN)
+
+        def each(full):
+            for link, there in links:
+                pl.when(there)(lambda: do(s.message(link, t, full)))
+
+        pl.when(valid & middle)(lambda: each(True))
+        pl.when(valid & jnp.logical_not(middle) & (t < STEPS - D))(lambda: each(False))
 
     def outs(s, b):
         k, q = lax.rem(b, NR), lax.rem(b, 8)
@@ -170,8 +169,9 @@
         s.H[k] = s.H[k] + s.PT[lax.rem(b, 4)].astype(f32)
 
     def service(s, t):
-        s.messages(t - D, t >= D, lambda c: c.wait_recv(), s.has_l, s.has_r)
-        s.messages(t - NS, t >= NS, lambda c: c.wait_send(), s.has_r, s.has_l)
+        always = t >= 0
+        s.messages(t - NS, t >= NS, lambda c: c.wait_send(), (2, always), (0, s.has_r), (1, s.has_l))
+        s.messages(t - D, t >= D, lambda c: c.wait_recv(), (2, always), (0, s.has_l), (1, s.has_r))
 
         def f(o):
             return lax.rem(t - o + 4 * NR, NR)
@@ -202,39 +202,34 @@
         SL[:, : 3 * L], SL[:, 11 * L :] = to_l, f3
         SY[:, 8 * L : 11 * L], SY[:, 11 * L :] = f0, f3
         hr, hl = h(D * z), h(D * zm)
+        here, at = pl.ds(s.bz, BT), pl.ds(pl.multiple_of(s.bz - BO + A2, L), BT)
+        H[hr, :, here] = H[hr, :, here] + jnp.where(s.has_l, RR[:, at].astype(f32), 0.0)
+        H[hl, :, here] = H[hl, :, here] + jnp.where(s.has_r, RL[:, at].astype(f32), 0.0)
         for q in range(4):
             b = pl.ds(BO + q * BT, BT)
-            m = pl.ds(3 * L + q * BT, BT)
-            rr, rl = RR[:, m], RL[:, m]
-            sum_r = H[hr, :, b] + jnp.where(s.has_l, rr.astype(f32), 0.0)
-
-            @pl.when(z == q)
-            def _():
-                H[hr, :, b] = sum_r
-
-            sum_l = H[hl, :, b] + jnp.where(s.has_r, rl.astype(f32), 0.0)
-
-            @pl.when(z == q)
-            def _():
-                H[hl, :, b] = sum_l
-
+            m = pl.ds(A2 + q * BT, BT)
             fq = f(5 * D + D * jnp.abs(z - q))
-
-            @pl.when(z > q)
-            def _():
-                F[fq, :, b] = rr
-
-            @pl.when(z < q)
-            def _():
-                F[fq, :, b] = rl
-
             done = F[fq, :, b]
-            SR[:, m] = jnp.where(z >= q, done, sum_r.astype(bf))
-            SL[:, m] = jnp.where(z <= q, done, sum_l.astype(bf))
+            if q < 3:
+                done = jnp.where(z > q, RR[:, m], done)
+            if q > 0:
+                done = jnp.where(z < q, RL[:, m], done)
+            F[fq, :, b] = done
+            if q > 0:
+                sum_r = H[hr, :, b] + jnp.where(s.has_l, RR[:, m].astype(f32), 0.0)
+                SR[:, m] = jnp.where(z < q, sum_r.astype(bf), done)
+            else:
+                SR[:, m] = done
+            if q < 3:
+                sum_l = H[hl, :, b] + jnp.where(s.has_r, RL[:, m].astype(f32), 0.0)
+                SL[:, m] = jnp.where(z > q, sum_l.astype(bf), done)
+            else:
+                SL[:, m] = done
+        s.messages(t, always, lambda c: c.start(), (0, s.has_r), (1, s.has_l))
         SY[:, : 6 * L] = H[h(0), :, pl.ds(s.o0, A)].astype(bf)
         SY[:, 6 * L : 7 * L] = H[h(3 * D), :, pl.ds(s.b_oth, L)].astype(bf)
         SY[:, 7 * L : 8 * L] = F[f(4 * D), :, pl.ds(s.b_own, L)]
-        s.messages(t, t >= 0, lambda c: c.start(), s.has_r, s.has_l)
+        s.messages(t, always, lambda c: c.start(), (2, always))
 
         @pl.when(t >= 8 * D)
         def _():
@@ -257,9 +252,9 @@
         for b in range(NB - W, NB):
             s.wait_outs(b)
         for t in range(STEPS - D - NS + D, STEPS - D):
-            s.message(2, t, 2).wait_send()
-            pl.when(s.has_r)(lambda t=t: s.message(0, t, 2).wait_send())
-            pl.when(s.has_l)(lambda t=t: s.message(1, t, 2).wait_send())
+            s.message(2, t, False).wait_send()
+            pl.when(s.has_r)(lambda t=t: s.message(0, t, False).wait_send())
+            pl.when(s.has_l)(lambda t=t: s.message(1, t, False).wait_send())
 
 
     def weights(s):
@@ -321,13 +316,14 @@
         for j in range(2):
             s.to_partner(g, j).wait_recv()
 
-    def hidden(s, g, lo, hi):
+    def hidden(s, g, lo, hi, arrive=None):
         k = lax.rem(g, 2)
         rows = pl.ds(pl.multiple_of(g * G, G), G)
-        d = sum(
-            dot(s.POOL[s.dy_part(g, j), 0:Q], s.WD[lo:hi, j * Q : (j + 1) * Q], 1, 1)
-            for j in range(4)
-        )
+        d = 0.0
+        for j in range(4):
+            if arrive:
+                arrive(j)
+            d += dot(s.POOL[s.dy_part(g, j), 0:Q], s.WD[lo:hi, j * Q : (j + 1) * Q], 1, 1)
         a, u = s.GA[k, :, lo:hi].astype(f32), s.UP[k, :, lo:hi].astype(f32)
         sig = jax.nn.sigmoid(a)
         silu = a * sig
@@ -364,7 +360,7 @@
         @pl.when((r == 0) & (g + 1 < NG))
         def _():
             for c in s.group_loads(g + 1):
-                c.start()
+                c.start(priority=1)
 
     def piece1(s, u):
         g, r = u // PPG, lax.rem(u, PPG)
@@ -372,17 +368,22 @@
 
         @pl.when(r == 0)
         def _():
-            for n, c in enumerate(s.group_loads(g)):
-                c.wait()
-                if n < 4:
-
-                    @pl.when(g == 0)
-                    def _(n=n):
-                        first[n].wait()
-                        for c in quarters[n]:
-                            c.start()
-
-            s.hidden(g, 0, F0)
+            copies = s.group_loads(g)
+
+            def arrive(n):
+                copies[n].wait()
+
+                @pl.when(g == 0)
+                def _():
+                    first[n].wait()
+                    for c in quarters[n]:
+                        c.start(priority=1)
+
+                if n == 3:
+                    copies[4].wait()
+                    copies[5].wait()
+
+            s.hidden(g, 0, F0, arrive)
 
         pl.when(r == 1)(lambda: s.hidden(g, F0, FF))
         for j in range(4):
@@ -426,14 +427,9 @@
     def piece2(s, u):
         m = u - P2
 
-        @pl.when(m == 0)
-        def _():
-            s.x_tile(0)[1].start()
-            s.y_tile(0)[1].start()
-
         @pl.when(m < NX)
         def _():
-            pl.when(m + 1 < NX)(lambda: s.x_tile(m + 1)[1].start())
+            pl.when(m + 1 < NX)(lambda: s.x_tile(m + 1)[1].start(priority=1))
             tile, load = s.x_tile(m)
             load.wait()
             rows = pl.ds(pl.multiple_of(m * XT, XT), XT)
@@ -442,8 +438,8 @@
         @pl.when((m >= NX) & (m < NX + WIDE))
         def _():
             q = m - NX
-            pl.when(q + 1 < WIDE)(lambda: s.y_tile(q + 1)[1].start())
-            pl.when(q + 1 == WIDE)(lambda: s.half_tile(0)[1].start())
+            pl.when(q + 1 < WIDE)(lambda: s.y_tile(q + 1)[1].start(priority=1))
+            pl.when(q + 1 == WIDE)(lambda: s.half_tile(0)[1].start(priority=1))
             tile, load = s.y_tile(q)
             load.wait()
             columns = pl.ds(pl.multiple_of(q * YT, YT), YT)
@@ -452,7 +448,7 @@
         @pl.when(m >= NX + WIDE)
         def _():
             q = m - NX - WIDE
-            pl.when(m + 1 < PIECES2)(lambda: s.half_tile(q + 1)[1].start())
+            pl.when(m + 1 < PIECES2)(lambda: s.half_tile(q + 1)[1].start(priority=1))
             tile, load = s.half_tile(q)
             load.wait()
             n = YT // 2
@@ -472,6 +468,12 @@
         def iteration(u, _):
             pl.when(u <= P2)(lambda: s.before1(u))
             pl.when(u >= LEAD)(lambda: s.service(u - LEAD))
+
+            @pl.when(u == P2 - 3)
+            def _():
+                s.x_tile(0)[1].start(priority=1)
+                s.y_tile(0)[1].start(priority=1)
+
             pl.when(u < P2)(lambda: s.piece1(u))
             pl.when((u >= P2) & (u < P2 + PIECES2))(lambda: s.piece2(u))
             return 0

time: 237 us -> 233 us (0.983)
  Pallas kernels: 236 us -> 232 us
    pallas_call x1, Pallas kernels: 214 us -> 209 us  [step(): pl.pallas_call(lambda *refs: Kernel(*refs).run(), out_shape=[shape((T_ROW...]
where the time goes in v3:
time: 233 us
  Pallas kernels  232 us (100%)
    pallas_call x1, Pallas kernels, step(): pl.pallas_call(lambda *refs: Kernel(*refs).run(), out_shape=[shape((T_ROW...  209 us
    pallas_call x1, Pallas kernels, step(): pl.pallas_call(copy_out, out_shape=[shape((T_ROWS, D_MODEL), bf), shape((...  22.5 us

profile of v3, /device:TPU:0, one launch (start us, length us, event | category | flops | bytes accessed | tf_op | source)
XLA Modules:
  0.0 232.6 jit_solution(11140377089417581129)
XLA Ops:
  0.6 209.4 %mlp_backward.1 = (bf16[2048,5120]{1,0:T(8,128)(2,1)}, bf16[5120,1792]{1,0:T(8,128)(2,1)S(1)}, bf16[896,5120]{1,0:T(8,128)(2,1)S(1)}, f32[2048,2560]{1,0:T(8,128)}, bf16[2048,2560]{1,0:T(8,128)(2,1)}) custom-call(bf16[2048,5120]{1,0:T(8,128)(2,1)} %refs_0_.1, bf16[2048,5120]{1,0:T(8,128)(2,1)} %refs_1_.1, bf16[2048,896]{1,0:T(8,128)(2,1)} %refs_2_.1, ...), custom_call_target="tpu_custom_call" | custom-call | tf_op jit(solution)/shard_map/mlp_backward/pallas_call | solution.py:531
  210.1 22.5 %copy_out.1 = (bf16[2048,5120]{1,0:T(8,128)(2,1)}, bf16[5120,896]{1,0:T(8,128)(2,1)}, bf16[5120,896]{1,0:T(8,128)(2,1)}, bf16[896,5120]{1,0:T(8,128)(2,1)}) custom-call(bf16[2048,5120]{1,0:T(8,128)(2,1)} %get-tuple-element.7.dx, bf16[5120,1792]{1,0:T(8,128)(2,1)S(1)} %get-tuple-element.8.dwgu, bf16[896,5120]{1,0:T(8,128)(2,1)S(1)} %get-tuple-element.9.dwd), custom_call_target="tpu_custom_call" | custom-call | tf_op jit(solution)/shard_map/copy_out/pallas_call | solution.py:548

commit v4 on v3

--- a/solution.py
+++ b/solution.py
@@ -82,15 +82,17 @@
         i = lax.axis_index("tp")
         s.y, s.z, s.c = i // 8, lax.rem(i // 2, 4), lax.rem(i, 2)
         s.zm = 3 - s.z
-        s.yid, s.cid = i + 8 - 16 * s.y, i + 1 - 2 * s.c
-        s.rid, s.lid = jnp.minimum(i + 2, 15), jnp.maximum(i - 2, 0)
+        other = 1 - 2 * s.c
+        s.yid, s.cid = i + 8 - 16 * s.y + other, i + other
+        s.rid, s.lid = jnp.minimum(i + 2 + other, 15), jnp.maximum(i - 2 + other, 0)
+        s.side = lax.rem(s.c + s.y + s.z, 2)
         s.has_r, s.has_l = s.z < 3, s.z > 0
         m = pl.multiple_of
         s.a0, s.o0 = m(s.y * A, L), m((1 - s.y) * A, L)
         s.a3, s.o3 = m(s.a0 + A2, L), m(s.o0 + A2, L)
         s.bz = m(BO + s.z * BT, L)
         s.b_own, s.b_oth = m(s.bz + s.y * L, L), m(s.bz + (1 - s.y) * L, L)
-        s.half = m(s.c * HC, HC)
+        s.half = m(s.side * HC, HC)
 
     def barrier(s):
         b = pltpu.get_barrier_semaphore()
@@ -276,7 +278,7 @@
         return first, quarters
 
     def quarter(s, j):
-        mine = jnp.where(j < 2, 1 - s.c, s.c)
+        mine = jnp.where(j < 2, 1 - s.side, s.side)
         return pl.multiple_of(mine * HC + lax.rem(j, 2) * Q, Q)
 
     def dy_part(s, g, j):
@@ -356,6 +358,10 @@
                 for j in range(2):
                     s.H[b, :, j * Q : (j + 1) * Q] = s.OST[j, b * R : (b + 1) * R, :]
             s.chip_sum(jnp.int32(0))
+
+        @pl.when((u == LEAD) & (s.side == 1))
+        def _():
+            pl.delay(700)
 
         @pl.when((r == 0) & (g + 1 < NG))
         def _():

time: 233 us -> 228 us (0.979)
  Pallas kernels: 232 us -> 227 us
    pallas_call x1, Pallas kernels: 209 us -> 204 us  [step(): pl.pallas_call(lambda *refs: Kernel(*refs).run(), out_shape=[shape((T_ROW...]
where the time goes in v4:
time: 228 us
  Pallas kernels  227 us (100%)
    pallas_call x1, Pallas kernels, step(): pl.pallas_call(lambda *refs: Kernel(*refs).run(), out_shape=[shape((T_ROW...  204 us
    pallas_call x1, Pallas kernels, step(): pl.pallas_call(copy_out, out_shape=[shape((T_ROWS, D_MODEL), bf), shape((...  22.5 us

profile of v4, /device:TPU:0, one launch (start us, length us, event | category | flops | bytes accessed | tf_op | source)
XLA Modules:
  0.0 227.5 jit_solution(17841091887383083646)
XLA Ops:
  0.6 204.3 %mlp_backward.1 = (bf16[2048,5120]{1,0:T(8,128)(2,1)}, bf16[5120,1792]{1,0:T(8,128)(2,1)S(1)}, bf16[896,5120]{1,0:T(8,128)(2,1)S(1)}, f32[2048,2560]{1,0:T(8,128)}, bf16[2048,2560]{1,0:T(8,128)(2,1)}) custom-call(bf16[2048,5120]{1,0:T(8,128)(2,1)} %refs_0_.1, bf16[2048,5120]{1,0:T(8,128)(2,1)} %refs_1_.1, bf16[2048,896]{1,0:T(8,128)(2,1)} %refs_2_.1, ...), custom_call_target="tpu_custom_call" | custom-call | tf_op jit(solution)/shard_map/mlp_backward/pallas_call | solution.py:537
  205.0 22.5 %copy_out.1 = (bf16[2048,5120]{1,0:T(8,128)(2,1)}, bf16[5120,896]{1,0:T(8,128)(2,1)}, bf16[5120,896]{1,0:T(8,128)(2,1)}, bf16[896,5120]{1,0:T(8,128)(2,1)}) custom-call(bf16[2048,5120]{1,0:T(8,128)(2,1)} %get-tuple-element.7.dx, bf16[5120,1792]{1,0:T(8,128)(2,1)S(1)} %get-tuple-element.8.dwgu, bf16[896,5120]{1,0:T(8,128)(2,1)S(1)} %get-tuple-element.9.dwd), custom_call_target="tpu_custom_call" | custom-call | tf_op jit(solution)/shard_map/copy_out/pallas_call | solution.py:554

commit v5 on v4

--- a/solution.py
+++ b/solution.py
@@ -337,6 +337,11 @@
         rows = pl.ds(pl.multiple_of(g * G, G), G)
         return dot(s.DGU[rows, :], s.WGU[pl.ds(s.quarter(j), Q), :], 1, 1)
 
+    def direct(s, lo, hi):
+        for b in range(lo, hi):
+            for j in range(2):
+                s.H[b, :, j * Q : (j + 1) * Q] = s.OST[j, b * R : (b + 1) * R, :]
+
     def before1(s, u):
         g, r = u // PPG, lax.rem(u, PPG)
 
@@ -354,9 +359,7 @@
 
         @pl.when(u == LEAD)
         def _():
-            for b in range(DIRECT):
-                for j in range(2):
-                    s.H[b, :, j * Q : (j + 1) * Q] = s.OST[j, b * R : (b + 1) * R, :]
+            s.direct(0, 2)
             s.chip_sum(jnp.int32(0))
 
         @pl.when((u == LEAD) & (s.side == 1))
@@ -474,6 +477,7 @@
         def iteration(u, _):
             pl.when(u <= P2)(lambda: s.before1(u))
             pl.when(u >= LEAD)(lambda: s.service(u - LEAD))
+            pl.when(u == LEAD)(lambda: s.direct(2, DIRECT))
 
             @pl.when(u == P2 - 3)
             def _():
@@ -489,7 +493,7 @@
 
 
 XC, WC, YC = 16, 8, 8
-SLOTS, LAG = 6, 2
+SLOTS, LAG = 7, 2
 
 
 def copy_out(dx, dwgu, dwd, dx_out, dwg_out, dwu_out, dwd_out, mid, rd, wr, gs, us, ys):
@@ -569,7 +573,7 @@
                 DMA((WC,)),
                 DMA((YC,)),
             ],
-            compiler_params=pltpu.CompilerParams(vmem_limit_bytes=8 << 20),
+            compiler_params=pltpu.CompilerParams(vmem_limit_bytes=10 << 20),
             name="copy_out",
         )(dx, dw_gu, dw_down)
 

time: 228 us -> 228 us (level)
  no operation moved by 1% of the time
where the time goes in v5:
time: 228 us; the launch traced here: 227 us
  Pallas kernels  227 us (100%)
    pallas_call x1, Pallas kernels, step(): pl.pallas_call(lambda *refs: Kernel(*refs).run(), out_shape=[shape((T_ROW...  204 us
    pallas_call x1, Pallas kernels, step(): pl.pallas_call(copy_out, out_shape=[shape((T_ROWS, D_MODEL), bf), shape((...  22.4 us

profile of v5, /device:TPU:0, one launch (start us, length us, event | category | flops | bytes accessed | tf_op | source)
XLA Modules:
  0.0 227.4 jit_solution(4453333222659964169)
XLA Ops:
  0.6 204.4 %mlp_backward.1 = (bf16[2048,5120]{1,0:T(8,128)(2,1)}, bf16[5120,1792]{1,0:T(8,128)(2,1)S(1)}, bf16[896,5120]{1,0:T(8,128)(2,1)S(1)}, f32[2048,2560]{1,0:T(8,128)}, bf16[2048,2560]{1,0:T(8,128)(2,1)}) custom-call(bf16[2048,5120]{1,0:T(8,128)(2,1)} %refs_0_.1, bf16[2048,5120]{1,0:T(8,128)(2,1)} %refs_1_.1, bf16[2048,896]{1,0:T(8,128)(2,1)} %refs_2_.1, ...), custom_call_target="tpu_custom_call" | custom-call | tf_op jit(solution)/shard_map/mlp_backward/pallas_call | solution.py:541
  205.0 22.4 %copy_out.1 = (bf16[2048,5120]{1,0:T(8,128)(2,1)}, bf16[5120,896]{1,0:T(8,128)(2,1)}, bf16[5120,896]{1,0:T(8,128)(2,1)}, bf16[896,5120]{1,0:T(8,128)(2,1)}) custom-call(bf16[2048,5120]{1,0:T(8,128)(2,1)} %get-tuple-element.7.dx, bf16[5120,1792]{1,0:T(8,128)(2,1)S(1)} %get-tuple-element.8.dwgu, bf16[896,5120]{1,0:T(8,128)(2,1)S(1)} %get-tuple-element.9.dwd), custom_call_target="tpu_custom_call" | custom-call | tf_op jit(solution)/shard_map/copy_out/pallas_call | solution.py:558
